TPU v7x, 256 devices: a whole 4x4x8 slice. The times are simulated.
256 devices in a mesh: row: 64 (over x_hi, y, z), col: 4 (over x_lo, core).
Axes of the slice: x: 4 (x_hi: 2, x_lo: 2; x = x_hi * 2 + x_lo), y: 4, z: 8, core: 2. Of those that a mesh axis runs over, the one named last changes fastest.
Arguments:
- tables: bfloat16 [256, 8192, 256], P(('row', 'col')), may hold values from -1.78125 to 1.78125, as said below
- bags: int32 [256, 8, 1024], P('row'), may hold values from 0 to 8191
- old_map: int32 [256], replicated, may hold values from 0 to 255, each once
- new_map: int32 [256], replicated, may hold values from 0 to 255, each once
Outputs:
- features: bfloat16 [1024, 256, 256], P('row', None, 'col')
Inputs may be any that keep to these rules, and one draw needn't show every extreme that they name: `tables`: every entry is a whole multiple of 1/64. `old_map`: a permutation of the table ids. `new_map`: a permutation of the output positions.
All inputs are finite; a program needn't handle non-finite values. Where the computation divides by a largest or mean magnitude, that divisor is 1e-20 or more.
Results may differ from a plain program's by a relative error of at most 0.01.
Values may be sent and summed in bfloat16 or wider, within the bound.
A program may use at most 64 MiB of HBM per device.

v0:
```python
import jax
import jax.numpy as jnp
from jax import lax
from jax.sharding import PartitionSpec as P


def split_up(array, dim, peers):
    shape = array.shape
    pieces = array.reshape(*shape[:dim], peers, shape[dim] // peers, *shape[dim + 1 :])
    return jnp.moveaxis(pieces, dim, 0)


def laid_out(pieces, dim):
    pieces = jnp.moveaxis(pieces, 0, dim)
    shape = pieces.shape
    return pieces.reshape(*shape[:dim], shape[dim] * shape[dim + 1], *shape[dim + 2 :])


def exchange_both(array, axis, axes, splits, concats):
    sizes = [lax.axis_size(a) for a in axes]
    pieces = split_up(array, splits[0], sizes[0])
    pieces = jnp.moveaxis(split_up(pieces, splits[1] + 1, sizes[1]), 0, 1)
    inside = pieces.shape[2:]
    pieces = pieces.reshape(-1, *inside)
    pieces = lax.all_to_all(pieces, axis, split_axis=0, concat_axis=0, tiled=True)
    pieces = laid_out(pieces.reshape(*sizes, *inside), concats[0] + 1)
    return laid_out(pieces, concats[1])


def pool_gather(embedding, bag_rows):
    gathered = jnp.take(embedding, bag_rows, axis=0).astype(jnp.float32)
    return jnp.sum(gathered, axis=0)


def pool_all(stored, bag_rows):

    def pool_table(operands):
        return pool_gather(operands[0], operands[1])

    return lax.map(pool_table, (stored, bag_rows))


def quantize(pooled, piece_width):
    count, samples, width = pooled.shape
    pieces = pooled.reshape(count, samples, width // piece_width, piece_width)
    scale = jnp.max(jnp.abs(pieces), axis=3, keepdims=True) + 0.0078125
    levels = (
        jnp.floor(pieces * 127.0 / scale + 0.5).astype(jnp.bfloat16).reshape(count, samples, width)
    )
    return (levels, scale[:, :, :, 0])


def local(tables, bags, old_map, new_map):
    columns = lax.axis_size("col")
    piece_width = tables.shape[2] // columns
    stored = tables.shape[0]
    column_index = lax.axis_index("col")
    own_bags = lax.dynamic_slice_in_dim(bags, column_index * stored, stored, 0)
    pooled = pool_all(tables, own_bags)
    levels, scales = quantize(pooled, piece_width)
    moved, moved_scales = (
        exchange_both(levels, ("row", "col"), ("row", "col"), (1, 2), (0, 0)),
        exchange_both(
            scales.astype(jnp.bfloat16), ("row", "col"), ("row", "col"), (1, 2), (0, 0)
        ).astype(scales.dtype),
    )
    total = moved.shape[0]
    row_count = total // (columns * stored)
    arrived = moved.reshape(columns, row_count, stored, moved.shape[1], moved.shape[2])
    arrived = arrived.transpose(1, 0, 2, 3, 4).reshape(total, moved.shape[1], moved.shape[2])
    arrived_scales = moved_scales.reshape(columns, row_count, stored, moved_scales.shape[1], 1)
    arrived_scales = arrived_scales.transpose(1, 0, 2, 3, 4).reshape(
        total, moved_scales.shape[1], 1
    )
    restored = (arrived.astype(jnp.float32) * arrived_scales / 127.0).astype(jnp.bfloat16)
    position = new_map[old_map]
    result = jnp.zeros((restored.shape[1], restored.shape[0], restored.shape[2]), jnp.bfloat16)
    return result.at[:, position, :].set(jnp.swapaxes(restored, 0, 1))


def solution(mesh):
    return jax.shard_map(
        local,
        mesh=mesh,
        in_specs=(P(("row", "col"), None, None), P("row", None, None), P(), P()),
        out_specs=P("row", None, "col"),
        check_vma=False,
    )
```

profile of v0, /device:TPU:1, one launch (start us, length us, event | category | flops | bytes accessed | tf_op | source)
XLA Modules:
  0.0 106.3 jit_solution(18000055011661212908)
XLA Ops:
  0.0 0.0 copy-start
  0.0 0.8 fusion.3
  0.8 0.8 compare_and_fusion
  1.6 33.8 %gather_fusion.1 = bf16[8192,256]{1,0:T(8,128)(2,1)} fusion(bf16[8192,256]{1,0:T(8,128)(2,1)} %bitcast.31, s32[8192]{0:T(1024)S(1)} %bitcast_clamp_fusion), kind=kCustom, calls=%fused_computation.1 | custom fusion | bytes 8421376 | tf_op jit(solution)/shard_map/while/body/eval_jaxpr/jit(_take)/gather | solution.py:31
  35.3 3.7 %convert_reduce_fusion = f32[1024,256]{1,0:T(8,128)S(1)} fusion(bf16[8,1024,256]{2,1,0:T(8,128)(2,1)} %bitcast.32, pred[8,1024]{1,0:T(8,128)(4,1)S(1)} %compare_and_fusion), kind=kLoop, calls=%fused_computation.3 | loop fusion | flops 6029312 | bytes 5251072 | tf_op jit(solution)/shard_map/while/body/eval_jaxpr/reduce_sum | solution.py:32
  39.0 0.1 fusion.5
  39.1 0.3 copy.14
  39.5 0.1 bitcast_reduce_fusion
  39.6 0.1 convert_element_type.58
  39.7 0.1 copy.18
  39.8 0.8 copy.19
  40.5 15.6 %all-to-all-start.1 = ((bf16[256,1,16,1]{2,3,1,0:T(2,128)(2,1)}), bf16[256,1,16,1]{2,3,1,0:T(2,128)(2,1)S(1)}, u32[]{:S(2)}, u32[]{:S(2)}) async-start(bf16[256,1,16,1]{2,3,1,0:T(2,128)(2,1)} %copy.19), calls=%async_computation.1 | async-start | bytes 262144 | tf_op jit(solution)/shard_map/all_to_all | solution.py:25
  56.2 1.0 copy.21
  57.2 0.9 mul.28
  58.1 2.8 %fusion.2 = bf16[64,4,1,16,64]{4,1,3,0,2:T(4,128)(2,1)S(1)} fusion(f32[64,1,16,4,64]{4,3,2,0,1:T(4,128)S(1)} %mul.28, f32[64,16,4]{2,1,0:T(8,128)} %bitcast.34), kind=kLoop, calls=%fused_computation.9 | loop fusion | flops 1048576 | bytes 1589248 | tf_op jit(solution)/shard_map/transpose;transpose | solution.py:22
  60.9 0.0 copy-start.1
  60.9 0.3 copy.16
  61.2 1.3 %reshape.181 = bf16[256,2,512]{2,1,0:T(2,128)(2,1)} reshape(bf16[256,1,16,64]{3,2,1,0:T(8,128)(2,1)S(1)} %bitcast.33) | data formatting | bytes 1048576
  62.5 6.5 %all-to-all-done.1 = bf16[256,1,16,1]{2,3,1,0:T(2,128)(2,1)S(1)} async-done(((bf16[256,1,16,1]{2,3,1,0:T(2,128)(2,1)}), bf16[256,1,16,1]{2,3,1,0:T(2,128)(2,1)S(1)}, u32[]{:S(2)}, u32[]{:S(2)}) %all-to-all-start.1) | async-done | bytes 8224 | tf_op jit(solution)/shard_map/all_to_all | solution.py:25
  69.0 7.3 %all-to-all-start = ((bf16[256,2,512]{2,1,0:T(2,128)(2,1)}), bf16[256,2,512]{2,1,0:T(2,128)(2,1)S(1)}, u32[]{:S(2)}, u32[]{:S(2)}) async-start(bf16[256,2,512]{2,1,0:T(2,128)(2,1)} %reshape.181), calls=%async_computation | async-start | bytes 1048576 | tf_op jit(solution)/shard_map/all_to_all | solution.py:25
  76.2 0.0 copy-done.1
  76.3 0.0 copy-done
  76.3 1.9 %gather_fusion = s32[256]{0:T(256)S(1)} fusion(s32[256]{0:T(256)S(1)} %copy-done, s32[1024]{0:T(1024)S(1)} %pad_clamp_fusion), kind=kCustom, calls=%fused_computation | custom fusion | bytes 3072 | tf_op jit(solution)/shard_map/gather | solution.py:76
  78.3 0.1 convert_element_type.63
  78.4 17.7 %all-to-all-done = bf16[256,2,512]{2,1,0:T(2,128)(2,1)S(1)} async-done(((bf16[256,2,512]{2,1,0:T(2,128)(2,1)}), bf16[256,2,512]{2,1,0:T(2,128)(2,1)S(1)}, u32[]{:S(2)}, u32[]{:S(2)}) %all-to-all-start) | async-done | bytes 524320 | tf_op jit(solution)/shard_map/all_to_all | solution.py:25
  96.1 0.6 reshape.182
  96.7 0.7 fusion.1
  97.4 0.1 broadcast_in_dim.25
  97.6 7.1 %scatter_fusion = bf16[16,256,64]{2,0,1:T(8,128)(2,1)S(1)} fusion(bf16[16,256,64]{2,0,1:T(8,128)(2,1)S(1)} %broadcast_in_dim.25, s32[256]{0:T(256)S(1)} %bitcast.38, bf16[256,16,64]{2,1,0:T(8,128)(2,1)S(1)} %fusion.1), kind=kCustom, calls=%fused_computation.2 | custom fusion | bytes 1573888 | tf_op jit(solution)/shard_map/scatter | solution.py:78
  104.7 1.7 %copy.20 = bf16[16,256,64]{1,2,0:T(8,128)(2,1)} copy(bf16[16,256,64]{2,0,1:T(8,128)(2,1)S(1)} %scatter_fusion) | data formatting | bytes 1048576 | tf_op jit(solution)/shard_map/scatter | solution.py:78
  (5 shorter events, 0.0 us)
Async XLA Ops:
  0.0 76.3 %copy-start = (s32[256]{0:T(256)S(1)}, s32[256]{0:T(256)}, u32[]{:S(2)}) copy-start(s32[256]{0:T(256)} %param.7) | copy-start | bytes 3076
  40.5 28.5 %all-to-all-start.1 = ((bf16[256,1,16,1]{2,3,1,0:T(2,128)(2,1)}), bf16[256,1,16,1]{2,3,1,0:T(2,128)(2,1)S(1)}, u32[]{:S(2)}, u32[]{:S(2)}) async-start(bf16[256,1,16,1]{2,3,1,0:T(2,128)(2,1)} %copy.19), calls=%async_computation.1 | async-start | bytes 262144 | tf_op jit(solution)/shard_map/all_to_all | solution.py:25
  60.9 15.3 %copy-start.1 = (s32[256]{0:T(256)S(1)}, s32[256]{0:T(256)}, u32[]{:S(2)}) copy-start(s32[256]{0:T(256)} %param.6) | copy-start | bytes 3076
  69.0 27.1 %all-to-all-start = ((bf16[256,2,512]{2,1,0:T(2,128)(2,1)}), bf16[256,2,512]{2,1,0:T(2,128)(2,1)S(1)}, u32[]{:S(2)}, u32[]{:S(2)}) async-start(bf16[256,2,512]{2,1,0:T(2,128)(2,1)} %reshape.181), calls=%async_computation | async-start | bytes 1048576 | tf_op jit(solution)/shard_map/all_to_all | solution.py:25
where the time goes:
time: 107 us; the launch traced here: 106 us
  local copies, waits for them, and re-layouts  50 us (47%)
  waiting for transfers between devices  24.1 us (23%)
  starting transfers between devices  22.9 us (21%)
  other arithmetic  9.12 us (9%)
    gather x1, local copies, waits for them, and re-layouts, pool_gather(): gathered = jnp.take(embedding, bag_rows, axis=0).astype(jnp.float32)  33.8 us
    all_to_all x2, waiting for transfers between devices, exchange_both(): lax.all_to_all(pieces, axis, split_axis=0, concat_axis=0, tiled=True)  24.1 us
    all_to_all x2, starting transfers between devices, exchange_both(): lax.all_to_all(pieces, axis, split_axis=0, concat_axis=0, tiled=True)  22.9 us
    scatter x2, local copies, waits for them, and re-layouts, local(): return result.at[:, position, :].set(jnp.swapaxes(restored, 0, 1))  8.72 us
    reduce_sum x1, other arithmetic, pool_gather(): return jnp.sum(gathered, axis=0)  3.66 us
    another operation x1, other arithmetic, exchange_both(): pieces = jnp.moveaxis(split_up(pieces, splits[1] + 1, sizes[1]), 0, 1)  2.8 us
  transfers between devices with their start and end apart: 2, of which 2 were waited for; matrix products, arithmetic and copies ran while one was open for 8% of the time, Pallas kernels for 0%

commit v1 on v0

v1 whole, which is shorter than its diff:
```python
import functools

import jax
import jax.numpy as jnp
from jax import lax
from jax.experimental import pallas as pl
from jax.experimental.pallas import tpu as pltpu
from jax.sharding import PartitionSpec as P

MESH = pl.DeviceIdType.MESH
HIGH = 4096.0


def signed_step(index):
    half = lax.div(index + 1, 2)
    return jnp.where(lax.rem(index, 2) == 1, half, -half)


def pool_and_send(dims, bags_ref, table_ref, recv_ref, bags, raw, packed, pooled, send, bag_sem, table_sem, send_sem, recv_sem):
    rows, cols, per_row, pool, chunks = dims
    row, col = lax.axis_index("row"), lax.axis_index("col")
    me = row * cols + col
    total = rows * cols
    chunk = raw.shape[0] // chunks

    def table_copy(c):
        part = pl.ds(c * chunk, chunk)
        return pltpu.make_async_copy(table_ref.at[0, part, :], raw.at[part, :], table_sem.at[c])

    bag_copy = pltpu.make_async_copy(bags_ref.at[col], bags, bag_sem)
    bag_copy.start()
    for c in range(chunks):
        table_copy(c).start()

    barrier = pltpu.get_barrier_semaphore()

    def greet(i, _):
        other = lax.rem(me + i, total)
        pl.semaphore_signal(
            barrier, inc=1, device_id=(lax.div(other, cols), lax.rem(other, cols)), device_id_type=MESH
        )
        return 0

    lax.fori_loop(1, total, greet, 0)

    for c in range(chunks):
        table_copy(c).wait()

        def pack(i, _):
            at = pl.ds(pl.multiple_of(c * chunk + i * 64, 64), 64)
            pair = raw[at, :].astype(jnp.float32)
            packed[at, :] = pair[:, :128] + pair[:, 128:] * HIGH
            return 0

        lax.fori_loop(0, chunk // 64, pack, 0)
    bag_copy.wait()

    def destination(i):
        step = lax.rem(row + 1 + i, rows)
        return step

    def gather(i):
        base = destination(i) * per_row
        for j in range(per_row):
            total_row = packed[pl.ds(bags[0, base + j], 1), :]
            for l in range(1, pool):
                total_row = total_row + packed[pl.ds(bags[l, base + j], 1), :]
            pooled[pl.ds(j, 1), :] = total_row
        return pooled[0:8, :], pooled[8:16, :]

    def quantize(i, sums):
        first = lax.broadcasted_iota(jnp.int32, (8, 128), 1) < 64
        halves = []
        for s in sums:
            high = jnp.floor(s * (64.0 / HIGH) + 0.5)
            halves.append((s - high * (HIGH / 64.0), high * (1.0 / 64.0)))
        target = destination(i) * cols
        for k in range(4):
            top, bottom = halves[0][k // 2], halves[1][k // 2]
            if k % 2 == 0:
                block = jnp.where(first, top, pltpu.roll(bottom, 64, 1))
            else:
                block = jnp.where(first, pltpu.roll(top, 64, 1), bottom)
            size = jnp.abs(block)
            left = jnp.max(jnp.where(first, size, 0.0), axis=1, keepdims=True)
            right = jnp.max(jnp.where(first, 0.0, size), axis=1, keepdims=True)
            scale = jnp.where(first, left, right) + 0.0078125
            levels = jnp.floor(block * (127.0 / scale) + 0.5)
            send[target + k] = (levels * scale / 127.0).astype(jnp.bfloat16)

    def copy_to(r, k):
        return pltpu.make_async_remote_copy(
            src_ref=send.at[r * cols + k],
            dst_ref=recv_ref.at[me],
            send_sem=send_sem,
            recv_sem=recv_sem,
            device_id=(r, k),
            device_id_type=MESH,
        )

    def send_all(i):
        r = destination(i)
        for k in range(4):
            copy_to(r, k).start()

    sums = gather(0)
    quantize(0, sums)
    sums = gather(1)
    pl.semaphore_wait(barrier, total - 1)

    def body(i, sums):
        send_all(i - 2)
        quantize(i - 1, sums)
        return gather(i)

    sums = lax.fori_loop(2, rows, body, sums)
    send_all(rows - 2)
    quantize(rows - 1, sums)
    recv_ref[me] = send[me]
    for k in range(4):

        @pl.when(col != k)
        def _():
            copy_to(row, k).start()

    others = pl.ds(0, total - 1)
    done = pltpu.make_async_remote_copy(
        src_ref=send.at[others],
        dst_ref=recv_ref.at[others],
        send_sem=send_sem,
        recv_sem=recv_sem,
        device_id=(row, lax.rem(col + 1, cols)),
        device_id_type=MESH,
    )
    done.wait()


def place(old_ref, new_ref, recv_ref, out_ref, wide):
    total = recv_ref.shape[0]
    at = lax.broadcasted_iota(jnp.int32, (total, total), 0)
    new_hot = (at == new_ref[...]).astype(jnp.bfloat16)
    old_hot = (at == old_ref[...]).astype(jnp.bfloat16)
    moves = jnp.dot(new_hot, old_hot, preferred_element_type=jnp.float32).astype(jnp.bfloat16)
    wide[...] = recv_ref[...].astype(jnp.float32).reshape(wide.shape)
    for j in range(8):
        rows = wide[pl.ds(j, total, stride=8), :].astype(jnp.bfloat16)
        moved = lax.dot_general(
            rows, moves, (((0,), (1,)), ((), ())), preferred_element_type=jnp.float32
        ).astype(jnp.bfloat16)
        out_ref[j] = moved[:64]
        out_ref[j + 8] = moved[64:]


def solution(mesh):
    rows, cols = mesh.shape["row"], mesh.shape["col"]
    total = rows * cols

    def local(tables, bags, old_map, new_map):
        _, entries, width = tables.shape
        _, pool, batch = bags.shape
        per_row = batch // rows
        chunks = 8
        block = (total, 8, 128)
        recv = pl.pallas_call(
            functools.partial(pool_and_send, (rows, cols, per_row, pool, chunks)),
            out_shape=jax.ShapeDtypeStruct(block, jnp.bfloat16),
            in_specs=[pl.BlockSpec(memory_space=pl.ANY)] * 2,
            out_specs=pl.BlockSpec(memory_space=pltpu.VMEM),
            scratch_shapes=[
                pltpu.SMEM((pool, batch), jnp.int32),
                pltpu.VMEM((entries, width), jnp.bfloat16),
                pltpu.VMEM((entries, 128), jnp.float32),
                pltpu.VMEM((16, 128), jnp.float32),
                pltpu.VMEM(block, jnp.bfloat16),
                pltpu.SemaphoreType.DMA,
                pltpu.SemaphoreType.DMA((chunks,)),
                pltpu.SemaphoreType.DMA,
                pltpu.SemaphoreType.DMA,
            ],
            compiler_params=pltpu.CompilerParams(collective_id=0, has_side_effects=True),
        )(bags, tables)
        out = pl.pallas_call(
            place,
            out_shape=jax.ShapeDtypeStruct((per_row, width // cols, total), jnp.bfloat16),
            in_specs=[pl.BlockSpec(memory_space=pltpu.VMEM)] * 3,
            out_specs=pl.BlockSpec(memory_space=pltpu.VMEM),
            scratch_shapes=[pltpu.VMEM((total * 8, 128), jnp.float32)],
        )(old_map.reshape(1, total), new_map.reshape(1, total), recv)
        return jnp.swapaxes(out, 1, 2)

    return jax.shard_map(
        local,
        mesh=mesh,
        in_specs=(P(("row", "col"), None, None), P("row", None, None), P(), P()),
        out_specs=P("row", None, "col"),
        check_vma=False,
    )
```

time: 107 us -> 37.6 us (0.35)
  local copies, waits for them, and re-layouts: 50 us -> 0 us
  Pallas kernels: 0 us -> 37.5 us
  waiting for transfers between devices: 24.1 us -> 0 us
  starting transfers between devices: 22.9 us -> 0 us
  other arithmetic: 9.12 us -> 0 us
    pallas_call x0 -> x2, Pallas kernels: none -> 37.5 us  [the longest x1 35 us: local(): pl.pallas_call(functools.partial(pool_and_send, (rows, cols, per_row, poo...]
    gather x2 -> x0, local copies, waits for them, and re-layouts: 35.7 us -> none  [the longest x1 33.8 us: pool_gather(): gathered = jnp.take(embedding, bag_rows, axis=0).astype(jnp.float32)]
    all_to_all x2 -> x0, waiting for transfers between devices: 24.1 us -> none  [exchange_both(): lax.all_to_all(pieces, axis, split_axis=0, concat_axis=0, tiled=True)]
    all_to_all x2 -> x0, starting transfers between devices: 22.9 us -> none  [exchange_both(): lax.all_to_all(pieces, axis, split_axis=0, concat_axis=0, tiled=True)]
    scatter x2 -> x0, local copies, waits for them, and re-layouts: 8.72 us -> none  [local(): return result.at[:, position, :].set(jnp.swapaxes(restored, 0, 1))]
    reduce_sum x1 -> x0, other arithmetic: 3.66 us -> none  [pool_gather(): return jnp.sum(gathered, axis=0)]
    another operation x1 -> x0, other arithmetic: 2.8 us -> none  [exchange_both(): pieces = jnp.moveaxis(split_up(pieces, splits[1] + 1, sizes[1]), 0, 1)]
    unnamed x6 -> x0, local copies, waits for them, and re-layouts: 1.98 us -> none
  transfers between devices with their start and end apart: 2 -> 0, of which waited for: 2 -> 0; matrix products, arithmetic and copies ran while one was open for 8% -> 0% of each run, Pallas kernels for 0% -> 0%
where the time goes in v1:
time: 37.6 us; the launch traced here: 37.5 us
  Pallas kernels  37.5 us (100%)
    pallas_call x1, Pallas kernels, local(): pl.pallas_call(functools.partial(pool_and_send, (rows, cols, per_row, poo...  35 us
    pallas_call x1, Pallas kernels, local(): pl.pallas_call(place, out_shape=jax.ShapeDtypeStruct((per_row, width // c...  2.54 us

profile of v1, /device:TPU:1, one launch (start us, length us, event | category | flops | bytes accessed | tf_op | source)
XLA Modules:
  0.0 37.5 jit_solution(10459873747052579663)
XLA Ops:
  0.0 35.0 %shard_map.46.recv_ref = bf16[256,8,128]{2,1,0:T(8,128)(2,1)} custom-call(s32[4,8,1024]{2,1,0:T(8,128)} %bags_ref.1, bf16[1,8192,256]{2,1,0:T(8,128)(2,1)} %table_ref.1), custom_call_target="tpu_custom_call" | custom-call | tf_op jit(solution)/shard_map/pallas_call | solution.py:164
  35.0 2.5 %shard_map.47 = bf16[16,64,256]{2,1,0:T(8,128)(2,1)} custom-call(s32[1,256]{1,0:T(1,128)} %bitcast.3, s32[1,256]{1,0:T(1,128)} %bitcast.4, bf16[256,8,128]{2,1,0:T(8,128)(2,1)} %shard_map.46.recv_ref), custom_call_target="tpu_custom_call" | custom-call | tf_op jit(solution)/shard_map/pallas_call | solution.py:182

commit v2 on v1

v2 whole, which is shorter than its diff:
```python
import functools

import jax
import jax.numpy as jnp
from jax import lax
from jax.experimental import pallas as pl
from jax.experimental.pallas import tpu as pltpu
from jax.sharding import PartitionSpec as P

MESH = pl.DeviceIdType.MESH
HIGH = 4096.0


def pool_and_send(dims, bags_ref, table_ref, recv_ref, bags, raw, packed, pooled, send, bag_sem, table_sem, send_sem, recv_sem):
    rows, cols, per_row, pool, chunks = dims
    row, col = lax.axis_index("row"), lax.axis_index("col")
    me = row * cols + col
    total = rows * cols
    chunk = raw.shape[0] // chunks

    def table_copy(c):
        part = pl.ds(c * chunk, chunk)
        return pltpu.make_async_copy(table_ref.at[0, part, :], raw.at[part, :], table_sem.at[c])

    count = bags.shape[0]
    bag_copy = pltpu.make_async_copy(bags_ref.at[pl.ds(col * count, count)], bags, bag_sem)
    bag_copy.start()
    for c in range(chunks):
        table_copy(c).start()

    barrier = pltpu.get_barrier_semaphore()

    def signal(r, k):
        pl.semaphore_signal(barrier, inc=1, device_id=(r, k), device_id_type=MESH)

    def greet(i, _):
        for k in range(cols):
            signal((row + i) & (rows - 1), k)
        return 0

    lax.fori_loop(1, rows, greet, 0)
    for d in range(1, cols):
        signal(row, (col + d) & (cols - 1))

    for c in range(chunks):
        table_copy(c).wait()

        def pack(i, _):
            at = pl.ds(pl.multiple_of(c * chunk + i * 256, 256), 256)
            pair = raw[at, :].astype(jnp.float32)
            packed[at, :] = pair[:, :128] + pair[:, 128:] * HIGH
            return 0

        lax.fori_loop(0, chunk // 256, pack, 0)
    bag_copy.wait()

    def destination(i):
        return (row + 1 + i) & (rows - 1)

    def copy_to(r, k):
        return pltpu.make_async_remote_copy(
            src_ref=send.at[r * cols + k],
            dst_ref=recv_ref.at[me],
            send_sem=send_sem,
            recv_sem=recv_sem,
            device_id=(r, k),
            device_id_type=MESH,
        )

    def send_pair(i):
        for half in range(2):
            for k in range(4):
                copy_to(destination(2 * i + half), k).start()

    def gather(i):
        for half in range(2):
            r = destination(2 * i + half)
            base = (r >> 3) * (pool * 128) + (r & 7) * per_row
            listed = [bags.at[pl.ds(base + l * 128, per_row)] for l in range(pool)]
            for j in range(per_row):
                parts = [packed[pl.ds(listed[l][j], 1), :] for l in range(pool)]
                while len(parts) > 1:
                    parts = [parts[n] + parts[n + 1] for n in range(0, len(parts), 2)]
                pooled[pl.ds(half * per_row + j, 1), :] = parts[0]
        return tuple(pooled[pl.ds(8 * n, 8), :] for n in range(4))

    def quantize(i, sums):
        first = lax.broadcasted_iota(jnp.int32, (8, 128), 1) < 64
        for half in range(2):
            parts = []
            for s in sums[2 * half : 2 * half + 2]:
                high = jnp.floor(s * (64.0 / HIGH) + 0.5)
                parts.append((s - high * (HIGH / 64.0), high * (1.0 / 64.0)))
            target = destination(2 * i + half) * cols
            for k in range(4):
                top, bottom = parts[0][k // 2], parts[1][k // 2]
                if k % 2 == 0:
                    block = jnp.where(first, top, pltpu.roll(bottom, 64, 1))
                else:
                    block = jnp.where(first, pltpu.roll(top, 64, 1), bottom)
                size = jnp.abs(block)
                left = jnp.max(jnp.where(first, size, 0.0), axis=1, keepdims=True)
                right = jnp.max(jnp.where(first, 0.0, size), axis=1, keepdims=True)
                scale = jnp.where(first, left, right) + 0.0078125
                levels = jnp.floor(block * (127.0 / scale) + 0.5)
                send[target + k] = (levels * scale / 127.0).astype(jnp.bfloat16)

    steps = rows // 2
    sums = gather(0)
    quantize(0, sums)
    sums = gather(1)
    pl.semaphore_wait(barrier, total - 1)

    def body(i, sums):
        send_pair(i - 2)
        quantize(i - 1, sums)
        return gather(i)

    sums = lax.fori_loop(2, steps, body, sums)
    send_pair(steps - 2)
    quantize(steps - 1, sums)
    recv_ref[me] = send[me]
    for k in range(4):
        copy_to(destination(rows - 2), k).start()
    for k in range(4):

        @pl.when(col != k)
        def _():
            copy_to(row, k).start()

    others = pl.ds(0, total - 1)
    done = pltpu.make_async_remote_copy(
        src_ref=send.at[others],
        dst_ref=recv_ref.at[others],
        send_sem=send_sem,
        recv_sem=recv_sem,
        device_id=(row, lax.rem(col + 1, cols)),
        device_id_type=MESH,
    )
    done.wait()


def place(old_ref, new_ref, recv_ref, out_ref, wide):
    total = recv_ref.shape[0]
    at = lax.broadcasted_iota(jnp.int32, (total, total), 0)
    new_hot = (at == new_ref[...]).astype(jnp.bfloat16)
    old_hot = (at == old_ref[...]).astype(jnp.bfloat16)
    moves = jnp.dot(new_hot, old_hot, preferred_element_type=jnp.float32).astype(jnp.bfloat16)
    wide[...] = recv_ref[...].astype(jnp.float32).reshape(wide.shape)
    for j in range(8):
        rows = wide[pl.ds(j, total, stride=8), :].astype(jnp.bfloat16)
        moved = lax.dot_general(
            rows, moves, (((0,), (1,)), ((), ())), preferred_element_type=jnp.float32
        ).astype(jnp.bfloat16)
        out_ref[j] = moved[:64]
        out_ref[j + 8] = moved[64:]


def solution(mesh):
    rows, cols = mesh.shape["row"], mesh.shape["col"]
    total = rows * cols

    def local(tables, bags, old_map, new_map):
        _, entries, width = tables.shape
        _, pool, batch = bags.shape
        per_row = batch // rows
        chunks = 8
        block = (total, 8, 128)
        listed = bags.reshape(cols, pool, batch // 128, 128).swapaxes(1, 2).reshape(-1)
        recv = pl.pallas_call(
            functools.partial(pool_and_send, (rows, cols, per_row, pool, chunks)),
            out_shape=jax.ShapeDtypeStruct(block, jnp.bfloat16),
            in_specs=[pl.BlockSpec(memory_space=pltpu.HBM)] * 2,
            out_specs=pl.BlockSpec(memory_space=pltpu.VMEM),
            scratch_shapes=[
                pltpu.SMEM((pool * batch,), jnp.int32),
                pltpu.VMEM((entries, width), jnp.bfloat16),
                pltpu.VMEM((entries, 128), jnp.float32),
                pltpu.VMEM((32, 128), jnp.float32),
                pltpu.VMEM(block, jnp.bfloat16),
                pltpu.SemaphoreType.DMA,
                pltpu.SemaphoreType.DMA((chunks,)),
                pltpu.SemaphoreType.DMA,
                pltpu.SemaphoreType.DMA,
            ],
            compiler_params=pltpu.CompilerParams(collective_id=0, has_side_effects=True, vmem_limit_bytes=16 << 20),
        )(pltpu.with_memory_space_constraint(listed, pltpu.HBM), pltpu.with_memory_space_constraint(tables, pltpu.HBM))
        out = pl.pallas_call(
            place,
            out_shape=jax.ShapeDtypeStruct((per_row, width // cols, total), jnp.bfloat16),
            in_specs=[pl.BlockSpec(memory_space=pltpu.VMEM)] * 3,
            out_specs=pl.BlockSpec(memory_space=pltpu.VMEM),
            scratch_shapes=[pltpu.VMEM((total * 8, 128), jnp.float32)],
            compiler_params=pltpu.CompilerParams(vmem_limit_bytes=16 << 20),
        )(old_map.reshape(1, total), new_map.reshape(1, total), recv)
        return jnp.swapaxes(out, 1, 2)

    return jax.shard_map(
        local,
        mesh=mesh,
        in_specs=(P(("row", "col"), None, None), P("row", None, None), P(), P()),
        out_specs=P("row", None, "col"),
        check_vma=False,
    )
```

time: 37.6 us -> 29.6 us (0.79)
  Pallas kernels: 37.5 us -> 29.5 us
    pallas_call x1, Pallas kernels: 35 us -> 28 us  [local(): pl.pallas_call(functools.partial(pool_and_send, (rows, cols, per_row, poo...]
    pallas_call x1, Pallas kernels: 2.54 us -> 1.47 us  [local(): pl.pallas_call(place, out_shape=jax.ShapeDtypeStruct((per_row, width // c...]
where the time goes in v2:
time: 29.6 us; the launch traced here: 29.5 us
  Pallas kernels  29.5 us (100%)
    pallas_call x1, Pallas kernels, local(): pl.pallas_call(functools.partial(pool_and_send, (rows, cols, per_row, poo...  28 us
    pallas_call x1, Pallas kernels, local(): pl.pallas_call(place, out_shape=jax.ShapeDtypeStruct((per_row, width // c...  1.47 us

profile of v2, /device:TPU:1, one launch (start us, length us, event | category | flops | bytes accessed | tf_op | source)
XLA Modules:
  0.0 29.5 jit_solution(17160613316432238855)
XLA Ops:
  0.0 0.0 copy-start.1
  0.0 0.0 copy-start
  0.0 28.0 %shard_map.46.recv_ref = bf16[256,8,128]{2,1,0:T(8,128)(2,1)S(1)} custom-call(s32[32768]{0:T(1024)} %bitcast.10, bf16[1,8192,256]{2,1,0:T(8,128)(2,1)} %table_ref.1), custom_call_target="tpu_custom_call" | custom-call | tf_op jit(solution)/shard_map/pallas_call | solution.py:170
  28.0 0.0 copy-done.1
  28.0 0.0 copy-done
  28.0 1.5 %shard_map.47 = bf16[16,64,256]{2,1,0:T(8,128)(2,1)} custom-call(s32[1,256]{1,0:T(1,128)S(1)} %bitcast.8, s32[1,256]{1,0:T(1,128)S(1)} %bitcast.9, bf16[256,8,128]{2,1,0:T(8,128)(2,1)S(1)} %shard_map.46.recv_ref), custom_call_target="tpu_custom_call" | custom-call | tf_op jit(solution)/shard_map/pallas_call | solution.py:188
Async XLA Ops:
  0.0 28.0 %copy-start.1 = (s32[256]{0:T(256)S(1)}, s32[256]{0:T(256)}, u32[]{:S(2)}) copy-start(s32[256]{0:T(256)} %param.7) | copy-start | bytes 3076
  0.0 28.0 %copy-start = (s32[256]{0:T(256)S(1)}, s32[256]{0:T(256)}, u32[]{:S(2)}) copy-start(s32[256]{0:T(256)} %param.6) | copy-start | bytes 3076

commit v3 on v2

--- a/solution.py
+++ b/solution.py
@@ -11,7 +11,7 @@
 HIGH = 4096.0
 
 
-def pool_and_send(dims, bags_ref, table_ref, recv_ref, bags, raw, packed, pooled, send, bag_sem, table_sem, send_sem, recv_sem):
+def pool_and_send(dims, bags_ref, table_ref, recv_ref, bags, raw, packed, pooled, send, bag_sem, table_sem, send_sem, recv_sem, class_sem):
     rows, cols, per_row, pool, chunks = dims
     row, col = lax.axis_index("row"), lax.axis_index("col")
     me = row * cols + col
@@ -33,14 +33,29 @@
     def signal(r, k):
         pl.semaphore_signal(barrier, inc=1, device_id=(r, k), device_id_type=MESH)
 
+    z, y = row & 7, (row >> 3) & 3
+    own_class = jnp.where(z < 4, z >> 1, 2 + (y >> 1))
+
     def greet(i, _):
-        for k in range(cols):
-            signal((row + i) & (rows - 1), k)
+        signal((row + i) & (rows - 1), own_class)
         return 0
 
-    lax.fori_loop(1, rows, greet, 0)
+    lax.fori_loop(1, rows, greet, 0, unroll=3)
     for d in range(1, cols):
         signal(row, (col + d) & (cols - 1))
+
+    def class_is_in(c):
+        @pl.when(col == c)
+        def _():
+            pl.semaphore_wait(barrier, jnp.where(own_class == c, total // 4 - 1, total // 4 + cols - 1))
+            for d in range(1, cols):
+                pl.semaphore_signal(
+                    class_sem.at[c], inc=1, device_id=(row, (c + d) % cols), device_id_type=MESH
+                )
+
+        @pl.when(col != c)
+        def _():
+            pl.semaphore_wait(class_sem.at[c], 1)
 
     for c in range(chunks):
         table_copy(c).wait()
@@ -55,26 +70,32 @@
     bag_copy.wait()
 
     def destination(i):
-        return (row + 1 + i) & (rows - 1)
-
-    def copy_to(r, k):
-        return pltpu.make_async_remote_copy(
+        c, u = i >> 4, i & 15
+        near = (u >> 1) * 8 + c * 2 + ((u + z) & 1)
+        far = (u >> 3) * 32 + (c & 1) * 16 + ((u >> 2) & 1) * 8 + 4 + ((u + z) & 3)
+        return jnp.where(i < rows // 2, near, far)
+
+    def pair(p):
+        return destination(2 * p), destination(2 * p + 1)
+
+    def send_to(r, k):
+        own = (r == row) & (col == k)
+        pltpu.make_async_remote_copy(
             src_ref=send.at[r * cols + k],
-            dst_ref=recv_ref.at[me],
+            dst_ref=recv_ref.at[jnp.where(own, total, me)],
             send_sem=send_sem,
             recv_sem=recv_sem,
-            device_id=(r, k),
+            device_id=(r, jnp.where(own, k ^ 1, k)),
             device_id_type=MESH,
-        )
-
-    def send_pair(i):
-        for half in range(2):
-            for k in range(4):
-                copy_to(destination(2 * i + half), k).start()
-
-    def gather(i):
-        for half in range(2):
-            r = destination(2 * i + half)
+        ).start()
+
+    def send_pair(targets):
+        for r in targets:
+            for k in range(cols):
+                send_to(r, k)
+
+    def gather(targets):
+        for half, r in enumerate(targets):
             base = (r >> 3) * (pool * 128) + (r & 7) * per_row
             listed = [bags.at[pl.ds(base + l * 128, per_row)] for l in range(pool)]
             for j in range(per_row):
@@ -84,14 +105,14 @@
                 pooled[pl.ds(half * per_row + j, 1), :] = parts[0]
         return tuple(pooled[pl.ds(8 * n, 8), :] for n in range(4))
 
-    def quantize(i, sums):
+    def quantize(targets, sums):
         first = lax.broadcasted_iota(jnp.int32, (8, 128), 1) < 64
         for half in range(2):
             parts = []
             for s in sums[2 * half : 2 * half + 2]:
                 high = jnp.floor(s * (64.0 / HIGH) + 0.5)
                 parts.append((s - high * (HIGH / 64.0), high * (1.0 / 64.0)))
-            target = destination(2 * i + half) * cols
+            target = targets[half] * cols
             for k in range(4):
                 top, bottom = parts[0][k // 2], parts[1][k // 2]
                 if k % 2 == 0:
@@ -106,29 +127,30 @@
                 send[target + k] = (levels * scale / 127.0).astype(jnp.bfloat16)
 
     steps = rows // 2
-    sums = gather(0)
-    quantize(0, sums)
-    sums = gather(1)
-    pl.semaphore_wait(barrier, total - 1)
-
-    def body(i, sums):
-        send_pair(i - 2)
-        quantize(i - 1, sums)
-        return gather(i)
-
-    sums = lax.fori_loop(2, steps, body, sums)
-    send_pair(steps - 2)
-    quantize(steps - 1, sums)
+    older, old = pair(0), pair(1)
+    sums = gather(older)
+    quantize(older, sums)
+    sums = gather(old)
+
+    def body(p, carry):
+        older, old, sums = carry
+        new = pair(p)
+        send_pair(older)
+        quantize(old, sums)
+        return old, new, gather(new)
+
+    carry = older, old, sums
+    for c in range(4):
+        class_is_in(c)
+        start = 2 + c * (steps // 4)
+        carry = lax.fori_loop(start, min(start + steps // 4, steps), body, carry)
+    older, old, sums = carry
+    send_pair(older)
+    quantize(old, sums)
     recv_ref[me] = send[me]
-    for k in range(4):
-        copy_to(destination(rows - 2), k).start()
-    for k in range(4):
-
-        @pl.when(col != k)
-        def _():
-            copy_to(row, k).start()
-
-    others = pl.ds(0, total - 1)
+    send_pair(old)
+
+    others = pl.ds(0, total)
     done = pltpu.make_async_remote_copy(
         src_ref=send.at[others],
         dst_ref=recv_ref.at[others],
@@ -141,12 +163,12 @@
 
 
 def place(old_ref, new_ref, recv_ref, out_ref, wide):
-    total = recv_ref.shape[0]
+    total = old_ref.shape[1]
     at = lax.broadcasted_iota(jnp.int32, (total, total), 0)
     new_hot = (at == new_ref[...]).astype(jnp.bfloat16)
     old_hot = (at == old_ref[...]).astype(jnp.bfloat16)
     moves = jnp.dot(new_hot, old_hot, preferred_element_type=jnp.float32).astype(jnp.bfloat16)
-    wide[...] = recv_ref[...].astype(jnp.float32).reshape(wide.shape)
+    wide[...] = recv_ref[:total].astype(jnp.float32).reshape(wide.shape)
     for j in range(8):
         rows = wide[pl.ds(j, total, stride=8), :].astype(jnp.bfloat16)
         moved = lax.dot_general(
@@ -169,7 +191,7 @@
         listed = bags.reshape(cols, pool, batch // 128, 128).swapaxes(1, 2).reshape(-1)
         recv = pl.pallas_call(
             functools.partial(pool_and_send, (rows, cols, per_row, pool, chunks)),
-            out_shape=jax.ShapeDtypeStruct(block, jnp.bfloat16),
+            out_shape=jax.ShapeDtypeStruct((total + 1, 8, 128), jnp.bfloat16),
             in_specs=[pl.BlockSpec(memory_space=pltpu.HBM)] * 2,
             out_specs=pl.BlockSpec(memory_space=pltpu.VMEM),
             scratch_shapes=[
@@ -182,6 +204,7 @@
                 pltpu.SemaphoreType.DMA((chunks,)),
                 pltpu.SemaphoreType.DMA,
                 pltpu.SemaphoreType.DMA,
+                pltpu.SemaphoreType.REGULAR((4,)),
             ],
             compiler_params=pltpu.CompilerParams(collective_id=0, has_side_effects=True, vmem_limit_bytes=16 << 20),
         )(pltpu.with_memory_space_constraint(listed, pltpu.HBM), pltpu.with_memory_space_constraint(tables, pltpu.HBM))

time: 29.6 us -> 28 us (0.946)
  Pallas kernels: 29.5 us -> 27.9 us
    pallas_call x1, Pallas kernels: 28 us -> 26.5 us  [local(): pl.pallas_call(functools.partial(pool_and_send, (rows, cols, per_row, poo...]
where the time goes in v3:
time: 28 us
  Pallas kernels  27.9 us (100%)
    pallas_call x1, Pallas kernels, local(): pl.pallas_call(functools.partial(pool_and_send, (rows, cols, per_row, poo...  26.5 us
    pallas_call x1, Pallas kernels, local(): pl.pallas_call(place, out_shape=jax.ShapeDtypeStruct((per_row, width // c...  1.47 us

profile of v3, /device:TPU:1, one launch (start us, length us, event | category | flops | bytes accessed | tf_op | source)
XLA Modules:
  0.0 28.0 jit_solution(5375933467187530392)
XLA Ops:
  0.0 0.0 copy-start.1
  0.0 0.0 copy-start
  0.0 26.5 %shard_map.46.recv_ref = bf16[257,8,128]{2,1,0:T(8,128)(2,1)S(1)} custom-call(s32[32768]{0:T(1024)} %bitcast.10, bf16[1,8192,256]{2,1,0:T(8,128)(2,1)} %table_ref.1), custom_call_target="tpu_custom_call" | custom-call | tf_op jit(solution)/shard_map/pallas_call | solution.py:192
  26.5 0.0 copy-done.1
  26.5 0.0 copy-done
  26.5 1.5 %shard_map.47 = bf16[16,64,256]{2,1,0:T(8,128)(2,1)} custom-call(s32[1,256]{1,0:T(1,128)S(1)} %bitcast.8, s32[1,256]{1,0:T(1,128)S(1)} %bitcast.9, bf16[257,8,128]{2,1,0:T(8,128)(2,1)S(1)} %shard_map.46.recv_ref), custom_call_target="tpu_custom_call" | custom-call | tf_op jit(solution)/shard_map/pallas_call | solution.py:211
Async XLA Ops:
  0.0 26.5 %copy-start.1 = (s32[256]{0:T(256)S(1)}, s32[256]{0:T(256)}, u32[]{:S(2)}) copy-start(s32[256]{0:T(256)} %param.7) | copy-start | bytes 3076
  0.0 26.5 %copy-start = (s32[256]{0:T(256)S(1)}, s32[256]{0:T(256)}, u32[]{:S(2)}) copy-start(s32[256]{0:T(256)} %param.6) | copy-start | bytes 3076

commit v4 on v3

--- a/solution.py
+++ b/solution.py
@@ -35,9 +35,10 @@
 
     z, y = row & 7, (row >> 3) & 3
     own_class = jnp.where(z < 4, z >> 1, 2 + (y >> 1))
+    members = (rows // 4,) * 4
 
     def greet(i, _):
-        signal((row + i) & (rows - 1), own_class)
+        signal((row + i) & (rows - 1), own_class ^ 2)
         return 0
 
     lax.fori_loop(1, rows, greet, 0, unroll=3)
@@ -45,15 +46,15 @@
         signal(row, (col + d) & (cols - 1))
 
     def class_is_in(c):
-        @pl.when(col == c)
+        @pl.when(col == c ^ 2)
         def _():
-            pl.semaphore_wait(barrier, jnp.where(own_class == c, total // 4 - 1, total // 4 + cols - 1))
+            pl.semaphore_wait(barrier, members[c] * cols + jnp.where(own_class == c, -1, cols - 1))
             for d in range(1, cols):
                 pl.semaphore_signal(
-                    class_sem.at[c], inc=1, device_id=(row, (c + d) % cols), device_id_type=MESH
+                    class_sem.at[c], inc=1, device_id=(row, ((c ^ 2) + d) % cols), device_id_type=MESH
                 )
 
-        @pl.when(col != c)
+        @pl.when(col != c ^ 2)
         def _():
             pl.semaphore_wait(class_sem.at[c], 1)
 
@@ -70,9 +71,8 @@
     bag_copy.wait()
 
     def destination(i):
-        c, u = i >> 4, i & 15
-        near = (u >> 1) * 8 + c * 2 + ((u + z) & 1)
-        far = (u >> 3) * 32 + (c & 1) * 16 + ((u >> 2) & 1) * 8 + 4 + ((u + z) & 3)
+        near = ((i >> 1) & 7) * 8 + ((i >> 4) << 1) + ((i + z) & 1)
+        far = ((i >> 3) & 1) * 32 + ((i >> 4) & 1) * 16 + ((i >> 2) & 1) * 8 + 4 + ((i + z) & 3)
         return jnp.where(i < rows // 2, near, far)
 
     def pair(p):
@@ -103,7 +103,7 @@
                 while len(parts) > 1:
                     parts = [parts[n] + parts[n + 1] for n in range(0, len(parts), 2)]
                 pooled[pl.ds(half * per_row + j, 1), :] = parts[0]
-        return tuple(pooled[pl.ds(8 * n, 8), :] for n in range(4))
+        return tuple(pooled[pl.ds(n, 8, stride=2), :] for n in (0, 1, 16, 17))
 
     def quantize(targets, sums):
         first = lax.broadcasted_iota(jnp.int32, (8, 128), 1) < 64
@@ -139,11 +139,12 @@
         quantize(old, sums)
         return old, new, gather(new)
 
-    carry = older, old, sums
+    carry, start = (older, old, sums), 2
     for c in range(4):
         class_is_in(c)
-        start = 2 + c * (steps // 4)
-        carry = lax.fori_loop(start, min(start + steps // 4, steps), body, carry)
+        stop = min(start + members[c] // 2, steps)
+        carry = lax.fori_loop(start, stop, body, carry)
+        start = stop
     older, old, sums = carry
     send_pair(older)
     quantize(old, sums)
@@ -162,20 +163,27 @@
     done.wait()
 
 
-def place(old_ref, new_ref, recv_ref, out_ref, wide):
+def place(old_ref, new_ref, recv_ref, out_ref, wide, placed, sems):
     total = old_ref.shape[1]
     at = lax.broadcasted_iota(jnp.int32, (total, total), 0)
     new_hot = (at == new_ref[...]).astype(jnp.bfloat16)
     old_hot = (at == old_ref[...]).astype(jnp.bfloat16)
     moves = jnp.dot(new_hot, old_hot, preferred_element_type=jnp.float32).astype(jnp.bfloat16)
     wide[...] = recv_ref[:total].astype(jnp.float32).reshape(wide.shape)
+    copies = []
     for j in range(8):
         rows = wide[pl.ds(j, total, stride=8), :].astype(jnp.bfloat16)
         moved = lax.dot_general(
             rows, moves, (((0,), (1,)), ((), ())), preferred_element_type=jnp.float32
         ).astype(jnp.bfloat16)
-        out_ref[j] = moved[:64]
-        out_ref[j + 8] = moved[64:]
+        placed[2 * j] = moved[:64]
+        placed[2 * j + 1] = moved[64:]
+        if j % 2 == 1:
+            part = pl.ds(2 * j - 2, 4)
+            copies.append(pltpu.make_async_copy(placed.at[part], out_ref.at[part], sems.at[j // 2]))
+            copies[-1].start()
+    for copy in copies:
+        copy.wait()
 
 
 def solution(mesh):
@@ -212,8 +220,12 @@
             place,
             out_shape=jax.ShapeDtypeStruct((per_row, width // cols, total), jnp.bfloat16),
             in_specs=[pl.BlockSpec(memory_space=pltpu.VMEM)] * 3,
-            out_specs=pl.BlockSpec(memory_space=pltpu.VMEM),
-            scratch_shapes=[pltpu.VMEM((total * 8, 128), jnp.float32)],
+            out_specs=pl.BlockSpec(memory_space=pl.ANY),
+            scratch_shapes=[
+                pltpu.VMEM((total * 8, 128), jnp.float32),
+                pltpu.VMEM((per_row, width // cols, total), jnp.bfloat16),
+                pltpu.SemaphoreType.DMA((4,)),
+            ],
             compiler_params=pltpu.CompilerParams(vmem_limit_bytes=16 << 20),
         )(old_map.reshape(1, total), new_map.reshape(1, total), recv)
         return jnp.swapaxes(out, 1, 2)

time: 28 us -> 27.2 us (0.971)
  Pallas kernels: 27.9 us -> 26.9 us
    pallas_call x1, Pallas kernels: 26.5 us -> 25.6 us  [local(): pl.pallas_call(functools.partial(pool_and_send, (rows, cols, per_row, poo...]
where the time goes in v4:
time: 27.2 us; the launch traced here: 27 us
  Pallas kernels  26.9 us (99%)
    pallas_call x1, Pallas kernels, local(): pl.pallas_call(functools.partial(pool_and_send, (rows, cols, per_row, poo...  25.6 us
    pallas_call x1, Pallas kernels, local(): pl.pallas_call(place, out_shape=jax.ShapeDtypeStruct((per_row, width // c...  1.37 us

profile of v4, /device:TPU:1, one launch (start us, length us, event | category | flops | bytes accessed | tf_op | source)
XLA Modules:
  0.0 27.0 jit_solution(4516156395857619670)
XLA Ops:
  0.0 0.0 copy-start.1
  0.0 0.0 copy-start
  0.0 25.6 %shard_map.46.recv_ref = bf16[257,8,128]{2,1,0:T(8,128)(2,1)S(1)} custom-call(s32[32768]{0:T(1024)} %bitcast.10, bf16[1,8192,256]{2,1,0:T(8,128)(2,1)} %table_ref.1), custom_call_target="tpu_custom_call" | custom-call | tf_op jit(solution)/shard_map/pallas_call | solution.py:200
  25.6 0.0 copy-done.1
  25.6 0.0 copy-done
  25.6 1.4 %shard_map.47 = bf16[16,64,256]{2,1,0:T(8,128)(2,1)} custom-call(s32[1,256]{1,0:T(1,128)S(1)} %bitcast.8, s32[1,256]{1,0:T(1,128)S(1)} %bitcast.9, bf16[257,8,128]{2,1,0:T(8,128)(2,1)S(1)} %shard_map.46.recv_ref), custom_call_target="tpu_custom_call" | custom-call | tf_op jit(solution)/shard_map/pallas_call | solution.py:219
Async XLA Ops:
  0.0 25.6 %copy-start.1 = (s32[256]{0:T(256)S(1)}, s32[256]{0:T(256)}, u32[]{:S(2)}) copy-start(s32[256]{0:T(256)} %param.7) | copy-start | bytes 3076
  0.0 25.6 %copy-start = (s32[256]{0:T(256)S(1)}, s32[256]{0:T(256)}, u32[]{:S(2)}) copy-start(s32[256]{0:T(256)} %param.6) | copy-start | bytes 3076

commit v5 on v4

--- a/solution.py
+++ b/solution.py
@@ -169,7 +169,7 @@
     new_hot = (at == new_ref[...]).astype(jnp.bfloat16)
     old_hot = (at == old_ref[...]).astype(jnp.bfloat16)
     moves = jnp.dot(new_hot, old_hot, preferred_element_type=jnp.float32).astype(jnp.bfloat16)
-    wide[...] = recv_ref[:total].astype(jnp.float32).reshape(wide.shape)
+    wide[: 8 * total] = recv_ref[:total].astype(jnp.float32).reshape(8 * total, 128)
     copies = []
     for j in range(8):
         rows = wide[pl.ds(j, total, stride=8), :].astype(jnp.bfloat16)
@@ -178,10 +178,9 @@
         ).astype(jnp.bfloat16)
         placed[2 * j] = moved[:64]
         placed[2 * j + 1] = moved[64:]
-        if j % 2 == 1:
-            part = pl.ds(2 * j - 2, 4)
-            copies.append(pltpu.make_async_copy(placed.at[part], out_ref.at[part], sems.at[j // 2]))
-            copies[-1].start()
+        part = pl.ds(2 * j, 2)
+        copies.append(pltpu.make_async_copy(placed.at[part], out_ref.at[part], sems.at[j]))
+        copies[-1].start()
     for copy in copies:
         copy.wait()
 
@@ -206,7 +205,7 @@
                 pltpu.SMEM((pool * batch,), jnp.int32),
                 pltpu.VMEM((entries, width), jnp.bfloat16),
                 pltpu.VMEM((entries, 128), jnp.float32),
-                pltpu.VMEM((32, 128), jnp.float32),
+                pltpu.VMEM((40, 128), jnp.float32),
                 pltpu.VMEM(block, jnp.bfloat16),
                 pltpu.SemaphoreType.DMA,
                 pltpu.SemaphoreType.DMA((chunks,)),
@@ -222,9 +221,9 @@
             in_specs=[pl.BlockSpec(memory_space=pltpu.VMEM)] * 3,
             out_specs=pl.BlockSpec(memory_space=pl.ANY),
             scratch_shapes=[
-                pltpu.VMEM((total * 8, 128), jnp.float32),
+                pltpu.VMEM((total * 8 + 8, 128), jnp.float32),
                 pltpu.VMEM((per_row, width // cols, total), jnp.bfloat16),
-                pltpu.SemaphoreType.DMA((4,)),
+                pltpu.SemaphoreType.DMA((8,)),
             ],
             compiler_params=pltpu.CompilerParams(vmem_limit_bytes=16 << 20),
         )(old_map.reshape(1, total), new_map.reshape(1, total), recv)

time: 27.2 us -> 27.2 us (level)
  no operation moved by 1% of the time
where the time goes in v5:
time: 27.2 us; the launch traced here: 27 us
  Pallas kernels  27 us (99%)
    pallas_call x1, Pallas kernels, local(): pl.pallas_call(functools.partial(pool_and_send, (rows, cols, per_row, poo...  25.6 us
    pallas_call x1, Pallas kernels, local(): pl.pallas_call(place, out_shape=jax.ShapeDtypeStruct((per_row, width // c...  1.41 us

profile of v5, /device:TPU:1, one launch (start us, length us, event | category | flops | bytes accessed | tf_op | source)
XLA Modules:
  0.0 27.0 jit_solution(11155308865545117347)
XLA Ops:
  0.0 0.0 copy-start.1
  0.0 0.0 copy-start
  0.0 25.6 %shard_map.46.recv_ref = bf16[257,8,128]{2,1,0:T(8,128)(2,1)S(1)} custom-call(s32[32768]{0:T(1024)} %bitcast.10, bf16[1,8192,256]{2,1,0:T(8,128)(2,1)} %table_ref.1), custom_call_target="tpu_custom_call" | custom-call | tf_op jit(solution)/shard_map/pallas_call | solution.py:199
  25.6 0.0 copy-done.1
  25.6 0.0 copy-done
  25.6 1.4 %shard_map.47 = bf16[16,64,256]{2,1,0:T(8,128)(2,1)} custom-call(s32[1,256]{1,0:T(1,128)S(1)} %bitcast.8, s32[1,256]{1,0:T(1,128)S(1)} %bitcast.9, bf16[257,8,128]{2,1,0:T(8,128)(2,1)S(1)} %shard_map.46.recv_ref), custom_call_target="tpu_custom_call" | custom-call | tf_op jit(solution)/shard_map/pallas_call | solution.py:218
Async XLA Ops:
  0.0 25.6 %copy-start.1 = (s32[256]{0:T(256)S(1)}, s32[256]{0:T(256)}, u32[]{:S(2)}) copy-start(s32[256]{0:T(256)} %param.7) | copy-start | bytes 3076
  0.0 25.6 %copy-start = (s32[256]{0:T(256)S(1)}, s32[256]{0:T(256)}, u32[]{:S(2)}) copy-start(s32[256]{0:T(256)} %param.6) | copy-start | bytes 3076
